TPU v7x, 128 devices: a whole 4x4x4 slice. The times are simulated.
128 devices in a mesh: tok: 8 (over z_lo, x), row: 4 (over z_hi, core), col: 4 (over y).
Axes of the slice: x: 4, y: 4, z: 4 (z_hi: 2, z_lo: 2; z = z_hi * 2 + z_lo), core: 2. Of those that a mesh axis runs over, the one named last changes fastest.
Arguments:
- activations: bfloat16 [2, 1024, 28672], P(None, 'tok', ('row', 'col')), may hold values from -0.1875 to 0.1875
- weights: bfloat16 [2, 28672, 8192], P(None, ('row', 'col'), 'tok'), may hold values from -6 to 6
Outputs:
- solved: float32 [256, 8192], P('row', ('tok', 'col'))
- correction: bfloat16 [28672, 8192], P(('row', 'col'), 'tok')
All inputs are finite; a program needn't handle non-finite values.
Results may differ from a plain program's by a relative error of at most 0.0073.
Values may be sent and summed in bfloat16 or wider, within the bound.
A program may use at most 64 MiB of HBM per device.

v0:
```python
import jax
import jax.numpy as jnp
from jax import lax
from jax.sharding import PartitionSpec as P

PANEL = 256


def broadcast(array, axis, root):
    return lax.dynamic_index_in_dim(lax.all_gather(array, axis), root, 0, keepdims=False)


def in_blocks(array, dim, peers):
    lengths = array.shape
    tiles = array.reshape(*lengths[:dim], peers, lengths[dim] // peers, *lengths[dim + 1 :])
    return jnp.moveaxis(tiles, dim, 0)


def summed_on_arrival(array, axis, dim):
    peers = lax.axis_size(axis)
    tiles = lax.all_to_all(in_blocks(array, dim, peers), axis, 0, 0, tiled=True)
    return jnp.sum(tiles, axis=0)


def joined_along(tiles, dim):
    tiles = jnp.moveaxis(tiles, 0, dim)
    lengths = tiles.shape
    return tiles.reshape(*lengths[:dim], lengths[dim] * lengths[dim + 1], *lengths[dim + 2 :])


def from_everyone(array, axis):
    peers = lax.axis_size(axis)
    return lax.all_to_all(
        jnp.broadcast_to(array[None], (peers, *array.shape)), axis, 0, 0, tiled=True
    )


def gather_directly(array, axis, dim):
    return joined_along(from_everyone(array, axis), dim)


def body(activations, weights):
    row_count = lax.axis_size("row")
    col_count = lax.axis_size("col")
    rows_here = activations.shape[2]
    panel_width = PANEL
    block_rows = panel_width // row_count
    out_here = weights.shape[2]
    block_cols = out_here // col_count
    first_row = lax.axis_index(("row", "col")) * rows_here
    panel_tokens = broadcast(activations[:, :, :panel_width], ("row", "col"), 0)
    partial_value = jnp.einsum(
        "mti,mtp->mip", activations, panel_tokens, preferred_element_type=jnp.float32
    )
    gram_sums = lax.psum(partial_value, "tok")
    row_ids = first_row + jnp.arange(rows_here, dtype=jnp.int32)[:, None]
    col_ids = jnp.arange(panel_width, dtype=jnp.int32)[None, :]
    on_diagonal = row_ids == col_ids
    regular = gram_sums * jnp.where(on_diagonal, 1.0, 0.9).astype(jnp.float32)[None]
    regular_bf16 = regular.astype(jnp.bfloat16)
    summed = regular[0] + regular[1]
    offset = jnp.int32(0)
    outputs = []
    for position in range(block_rows * lax.axis_size(("row", "col")) // block_rows):
        block_id = offset // block_rows + position
        tile_row = block_id // col_count
        tile_col = block_id % col_count
        gram_part = lax.dynamic_slice_in_dim(regular_bf16, tile_row * block_rows, block_rows, 2)
        weight_part = lax.dynamic_slice_in_dim(weights, tile_col * block_cols, block_cols, 2)
        outputs.append(
            jnp.einsum("mip,mio->po", gram_part, weight_part, preferred_element_type=jnp.float32)
        )
    right_block = summed_on_arrival(jnp.concatenate(outputs, axis=0), ("row", "col"), 0)
    diagonal_part = broadcast(summed[:panel_width], ("row", "col"), 0)
    factor = jnp.linalg.cholesky(diagonal_part)
    panel_factor = lax.linalg.triangular_solve(
        factor, summed, left_side=False, lower=True, transpose_a=True
    )
    row_index = lax.axis_index("row")
    whole_right = gather_directly(right_block, "row", 0)
    whole_solved = lax.linalg.triangular_solve(factor, whole_right, left_side=True, lower=True)
    solved = lax.dynamic_slice_in_dim(whole_solved, row_index * block_rows, block_rows, 0)
    solved_columns = lax.all_gather(solved, "col", axis=1, tiled=True)
    correction = jnp.dot(
        panel_factor,
        lax.all_gather(solved_columns, "row", axis=0, tiled=True),
        precision=lax.Precision.HIGHEST,
        preferred_element_type=jnp.float32,
    )
    return (solved, correction.astype(jnp.bfloat16))


def solution(mesh):
    in_specs = (P(None, "tok", ("row", "col")), P(None, ("row", "col"), "tok"))
    out_specs = (P("row", ("tok", "col")), P(("row", "col"), "tok"))
    return jax.shard_map(body, mesh=mesh, in_specs=in_specs, out_specs=out_specs, check_vma=False)
```

profile of v0, /device:TPU:1, one launch (start us, length us, event | category | flops | bytes accessed | tf_op | source)
XLA Modules:
  0.0 338.8 jit_solution(6505781074480112813)
XLA Ops:
  7.2 1.6 slice.77
  8.9 54.1 %all-gather.9.cloned.1.call-done = bf16[32,128,256]{2,1,0:T(8,128)(2,1)} async-done(((bf16[2,128,256]{2,1,0:T(8,128)(2,1)}), bf16[32,128,256]{2,1,0:T(8,128)(2,1)}) %all-gather.9.cloned.1.call-update) | async-done | bytes 2097168 | tf_op jit(solution)/shard_map/all_gather | solution.py:10
  62.9 3.7 %fusion.151 = f32[2,1792,256]{2,1,0:T(8,128)} fusion(bf16[2,128,1792]{2,1,0:T(8,128)(2,1)} %param.2, bf16[32,128,256]{2,1,0:T(8,128)(2,1)} %all-gather.9.cloned.1.call-done), kind=kOutput, calls=%fused_computation.101 | convolution fusion | flops 234881024 | bytes 4718592 | tf_op jit(solution)/shard_map/mti,mtp->mip/dot_general | solution.py:52
  67.0 94.8 %all-reduce.3.cloned.1.call-done = f32[2,1792,256]{2,1,0:T(8,128)} async-done(((f32[2,1792,256]{2,1,0:T(8,128)}), f32[2,1792,256]{2,1,0:T(8,128)}) %all-reduce.3.cloned.1.call-update) | async-done | bytes 3670032 | tf_op jit(solution)/shard_map/psum | solution.py:55
  161.8 3.8 %fusion.163 = (bf16[2,1792,256]{2,1,0:T(8,128)(2,1)}, f32[2,1792,256]{2,1,0:T(8,128)S(1)}) fusion(f32[2,1792,256]{2,1,0:T(8,128)} %all-reduce.3.cloned.1.call-done, f32[1792,256]{1,0:T(8,128)S(1)} %fusion.3), kind=kLoop, calls=%fused_computation.126 | loop fusion | flops 1835008 | bytes 11010048 | tf_op jit(solution)/shard_map/convert_element_type | solution.py:60
  165.8 1.6 copy-done
  168.4 2.1 fusion.39
  170.5 2.0 fusion.63
  172.5 2.1 fusion.87
  174.6 2.0 fusion.111
  176.6 2.3 fusion.45
  185.6 0.8 fusion.129
  186.3 25.9 %all_to_all.10 = f32[16,64,256]{2,1,0:T(8,128)S(1)} all-to-all(f32[16,64,256]{2,1,0:T(8,128)S(1)} %bitcast.111), channel_id=1, replica_groups=mesh['tok'=8,'row'=4,'col'=4] {'row','col'}, dimensions={0} | all-to-all | bytes 2097152 | tf_op jit(solution)/shard_map/all_to_all | solution.py:21
  213.0 5.3 %all-to-all-start.1 = ((f32[4,64,256]{2,1,0:T(8,128)}), f32[4,64,256]{2,1,0:T(8,128)S(1)}, u32[]{:S(2)}, u32[]{:S(2)}) async-start(f32[4,64,256]{2,1,0:T(8,128)} %broadcast_in_dim.21), calls=%async_computation.1 | async-start | bytes 524288 | tf_op jit(solution)/shard_map/all_to_all | solution.py:33
  218.3 6.5 %all-to-all-done.1 = f32[4,64,256]{2,1,0:T(8,128)S(1)} async-done(((f32[4,64,256]{2,1,0:T(8,128)}), f32[4,64,256]{2,1,0:T(8,128)S(1)}, u32[]{:S(2)}, u32[]{:S(2)}) %all-to-all-start.1) | async-done | bytes 262176 | tf_op jit(solution)/shard_map/all_to_all | solution.py:33
  224.9 5.5 %all-gather.5.cloned.1.call-done = f32[16,256,256]{2,1,0:T(8,128)} async-done(((f32[1,256,256]{2,1,0:T(8,128)}), f32[16,256,256]{2,1,0:T(8,128)}) %all-gather.5.cloned.1.call-update) | async-done | bytes 4194320 | tf_op jit(solution)/shard_map/all_gather | solution.py:10
  230.4 1.0 dynamic_slice.70
  231.5 1.0 fusion.150
  232.5 11.7 %cholesky.50 = f32[128,128]{1,0:T(8,128)S(1)} custom-call(f32[128,128]{1,0:T(8,128)S(1)} %cholesky.118), custom_call_target="Cholesky" | custom-call | tf_op jit(solution)/shard_map/jit(cholesky)/cholesky | solution.py:75
  244.2 9.8 %custom-call.16 = f32[1,128,128]{1,2,0:T(8,128)S(1)} custom-call(f32[1,128,128]{2,1,0:T(8,128)S(1)} %get-tuple-element.27), custom_call_target="InvertDiagBlocksLowerTriangular" | custom-call | tf_op jit(solution)/shard_map/jit(cholesky)/cholesky | solution.py:75
  254.5 11.7 %cholesky.105 = f32[128,128]{1,0:T(8,128)S(1)} custom-call(f32[128,128]{1,0:T(8,128)S(1)} %convolution_subtract_fusion.2), custom_call_target="Cholesky" | custom-call | tf_op jit(solution)/shard_map/jit(cholesky)/cholesky | solution.py:75
  268.4 4.2 %while.1 = (s32[]{:T(128)}, f32[256,256]{1,0:T(8,128)S(1)}, s32[2,2]{1,0:T(2,128)S(1)}, f32[2,128,128]{2,1,0:T(8,128)S(1)}, s32[]{:T(128)}) while((s32[]{:T(128)}, f32[256,256]{1,0:T(8,128)S(1)}, s32[2,2]{1,0:T(2,128)S(1)}, f32[2,128,128]{2,1,0:T(8,128)S(1)}, s32[]{:T(128)}) %tuple.29), condition=%wide.while_cond, body=%wide.while_body.sunk | while | flops 2 | bytes 131181 | solution.py:81
  269.2 1.3 bitcast_dynamic-update-slice_fusion.2
  271.2 1.3 bitcast_dynamic-update-slice_fusion.2
  272.6 19.7 %custom-call.17 = f32[2,128,128]{1,2,0:T(8,128)S(1)} custom-call(f32[2,128,128]{2,1,0:T(8,128)S(1)} %get-tuple-element.9), custom_call_target="InvertDiagBlocksLowerTriangular" | custom-call | tf_op jit(solution)/shard_map/triangular_solve | solution.py:81
  293.2 10.1 %all_gather.19 = f32[64,1024]{1,0:T(8,128)} all-gather(f32[64,256]{1,0:T(8,128)S(1)} %fusion.153), channel_id=1, replica_groups=mesh['tok'=8,'row'=4,'col'=4] {'col'}, dimensions={1}, use_global_device_ids=true | all-gather | bytes 327680 | tf_op jit(solution)/shard_map/all_gather | solution.py:83
  303.4 2.3 fusion.175
  305.7 1.0 fusion.132
  306.6 1.6 convolution_subtract_fusion
  308.2 1.0 fusion.158
  309.2 14.3 %all-gather.7.cloned.1.call-done = f32[256,1024]{1,0:T(8,128)} async-done(((f32[64,1024]{1,0:T(8,128)}), f32[256,1024]{1,0:T(8,128)}) %all-gather.7.cloned.1.call-update) | async-done | bytes 1048592 | tf_op jit(solution)/shard_map/all_gather | solution.py:86
  323.5 8.7 %convolution_convert_fusion = bf16[1792,1024]{1,0:T(8,128)(2,1)} fusion(f32[256,1024]{1,0:T(8,128)} %all-gather.7.cloned.1.call-done, f32[1792,128]{0,1:T(8,128)S(1)} %fusion.158, f32[1792,128]{0,1:T(8,128)S(1)} %fusion.132), kind=kOutput, calls=%fused_computation.2 | convolution fusion | flops 5639438336 | bytes 6553600 | tf_op jit(solution)/shard_map/dot_general | solution.py:84
  (55 shorter events, 12.7 us)
Async XLA Ops:
  7.2 55.7 %all-gather.9.cloned.1.call-start = ((), (), s32[]{:S(2)}) async-start(), calls=%async_computation.5 | async-start | bytes 2228224 | tf_op jit(solution)/shard_map/all_gather | solution.py:10
  8.8 153.0 %all-reduce.3.cloned.1.call-start = ((), (), s32[]{:S(2)}) async-start(), calls=%async_computation.2 | async-start | bytes 7340032 | tf_op jit(solution)/shard_map/psum | solution.py:55
  66.6 163.7 %all-gather.5.cloned.1.call-start = ((), (), s32[]{:S(2)}) async-start(), calls=%async_computation.3 | async-start | bytes 4456448 | tf_op jit(solution)/shard_map/all_gather | solution.py:10
  165.6 1.9 copy-start
  165.6 2.8 copy-start.1
  168.4 10.5 %slice-start = ((s8[7340032]{0:T(1024)(128)(4,1)}), s8[4194304]{0:T(1024)(128)(4,1)S(1)}, s32[]{:S(2)}) async-start(s8[7340032]{0:T(1024)(128)(4,1)} %bitcast.114), calls=%async_computation.6 | async-start | bytes 8388608
  172.5 6.5 %slice-start.1 = ((s8[7340032]{0:T(1024)(128)(4,1)}), s8[3145728]{0:T(1024)(128)(4,1)S(1)}, s32[]{:S(2)}) async-start(s8[7340032]{0:T(1024)(128)(4,1)} %bitcast.114), calls=%async_computation.7 | async-start | bytes 6291456
  213.0 11.8 %all-to-all-start.1 = ((f32[4,64,256]{2,1,0:T(8,128)}), f32[4,64,256]{2,1,0:T(8,128)S(1)}, u32[]{:S(2)}, u32[]{:S(2)}) async-start(f32[4,64,256]{2,1,0:T(8,128)} %broadcast_in_dim.21), calls=%async_computation.1 | async-start | bytes 524288 | tf_op jit(solution)/shard_map/all_to_all | solution.py:33
  218.3 105.2 %all-gather.7.cloned.1.call-start = ((), (), s32[]{:S(2)}) async-start(), calls=%async_computation.4 | async-start | bytes 1310720 | tf_op jit(solution)/shard_map/all_gather | solution.py:86
  293.2 12.4 %copy-start.2 = (f32[64,256]{1,0:T(8,128)}, f32[64,256]{1,0:T(8,128)S(1)}, u32[]{:S(2)}) copy-start(f32[64,256]{1,0:T(8,128)S(1)} %fusion.153) | copy-start | bytes 196612
Sparse Core Ops, SparseCore 0:
  11.0 51.8 all-gather.8
  66.8 95.0 all-reduce.2
  168.3 61.9 all-gather.4
  303.5 20.0 all-gather.6
where the time goes:
time: 339 us
  waiting for transfers between devices  175 us (52%)
  other arithmetic  61.4 us (18%)
  blocking collectives  36 us (11%)
  matrix products  35.1 us (10%)
  between operations  15.3 us (5%)
  local copies, waits for them, and re-layouts  10.1 us (3%)
  starting transfers between devices  5.42 us (2%)
    psum x1, waiting for transfers between devices, body(): gram_sums = lax.psum(partial_value, 'tok')  94.8 us
    all_gather x2, waiting for transfers between devices, broadcast(): lax.all_gather(array, axis)  59.5 us
    another operation x6, other arithmetic, body(): factor = jnp.linalg.cholesky(diagonal_part)  34 us
    all_to_all x1, blocking collectives, summed_on_arrival(): tiles = lax.all_to_all(in_blocks(array, dim, peers), axis, 0, 0, tiled=True)  25.9 us
    another operation x4, other arithmetic, body(): lax.linalg.triangular_solve(factor, whole_right, left_side=True, lower=True)  19.7 us
    dot_general x16, matrix products, body(): jnp.einsum('mip,mio->po', gram_part, weight_part, preferred_element_type=...  17.8 us
    all_gather x1, waiting for transfers between devices, body(): lax.all_gather(solved_columns, 'row', axis=0, tiled=True)  14.3 us
    all_gather x1, blocking collectives, body(): solved_columns = lax.all_gather(solved, 'col', axis=1, tiled=True)  10.1 us
  transfers between devices with their start and end apart: 5, of which 5 were waited for; matrix products, arithmetic and copies ran while one was open for 7% of the time, Pallas kernels for 0%

commit v1 on v0

--- a/solution.py
+++ b/solution.py
@@ -52,7 +52,7 @@
     partial_value = jnp.einsum(
         "mti,mtp->mip", activations, panel_tokens, preferred_element_type=jnp.float32
     )
-    gram_sums = lax.psum(partial_value, "tok")
+    gram_sums = jnp.sum(lax.all_gather(partial_value, "tok"), axis=0)
     row_ids = first_row + jnp.arange(rows_here, dtype=jnp.int32)[:, None]
     col_ids = jnp.arange(panel_width, dtype=jnp.int32)[None, :]
     on_diagonal = row_ids == col_ids

time: 339 us -> 550 us (1.62)
  waiting for transfers between devices: 175 us -> 373 us
  other arithmetic: 61.4 us -> 73.9 us
    all_gather x0 -> x1, waiting for transfers between devices: none -> 287 us  [body(): gram_sums = jnp.sum(lax.all_gather(partial_value, 'tok'), axis=0)]
    psum x1 -> x0, waiting for transfers between devices: 94.8 us -> none  [body(): gram_sums = lax.psum(partial_value, 'tok')]
    reduce_sum x0 -> x1, other arithmetic: none -> 12.8 us  [body(): gram_sums = jnp.sum(lax.all_gather(partial_value, 'tok'), axis=0)]
  transfers between devices with their start and end apart: 5 -> 5, of which waited for: 5 -> 5; matrix products, arithmetic and copies ran while one was open for 7% -> 4% of each run, Pallas kernels for 0% -> 0%
where the time goes in v1:
time: 550 us; the launch traced here: 549 us
  waiting for transfers between devices  373 us (68%)
  other arithmetic  73.9 us (13%)
  blocking collectives  35.4 us (6%)
  matrix products  31.7 us (6%)
  local copies, waits for them, and re-layouts  15.3 us (3%)
  between operations  15.2 us (3%)
    all_gather x1, waiting for transfers between devices, body(): gram_sums = jnp.sum(lax.all_gather(partial_value, 'tok'), axis=0)  287 us
    all_gather x2, waiting for transfers between devices, broadcast(): lax.all_gather(array, axis)  62.3 us
    another operation x6, other arithmetic, body(): factor = jnp.linalg.cholesky(diagonal_part)  34 us
    all_to_all x1, blocking collectives, summed_on_arrival(): tiles = lax.all_to_all(in_blocks(array, dim, peers), axis, 0, 0, tiled=True)  25.3 us
    another operation x4, other arithmetic, body(): lax.linalg.triangular_solve(factor, whole_right, left_side=True, lower=True)  19.7 us
    all_gather x1, waiting for transfers between devices, body(): lax.all_gather(solved_columns, 'row', axis=0, tiled=True)  17.3 us
    dot_general x16, matrix products, body(): jnp.einsum('mip,mio->po', gram_part, weight_part, preferred_element_type=...  15 us
    reduce_sum x1, other arithmetic, body(): gram_sums = jnp.sum(lax.all_gather(partial_value, 'tok'), axis=0)  12.8 us
  transfers between devices with their start and end apart: 5, of which 5 were waited for; matrix products, arithmetic and copies ran while one was open for 4% of the time, Pallas kernels for 0%

profile of v1, /device:TPU:1, one launch (start us, length us, event | category | flops | bytes accessed | tf_op | source)
XLA Modules:
  0.0 549.1 jit_solution(9039926788433031201)
XLA Ops:
  7.2 1.6 slice.77
  8.9 54.1 %all-gather.11.cloned.1.call-done = bf16[32,128,256]{2,1,0:T(8,128)(2,1)} async-done(((bf16[2,128,256]{2,1,0:T(8,128)(2,1)}), bf16[32,128,256]{2,1,0:T(8,128)(2,1)}) %all-gather.11.cloned.1.call-update) | async-done | bytes 2097168 | tf_op jit(solution)/shard_map/all_gather | solution.py:10
  62.9 3.7 fusion.151
  66.8 286.6 %all-gather.13.cloned.1.call-done = f32[16,1792,256]{2,1,0:T(8,128)} async-done(((f32[2,1792,256]{2,1,0:T(8,128)}), f32[16,1792,256]{2,1,0:T(8,128)}) %all-gather.13.cloned.1.call-update) | async-done | bytes 29360144 | tf_op jit(solution)/shard_map/all_gather | solution.py:55
  353.5 12.8 %reduce_sum.18 = f32[2,1792,256]{2,1,0:T(8,128)} reduce(f32[8,2,1792,256]{3,2,1,0:T(8,128)} %bitcast.112, f32[]{:T(128)} %constant.833.clone.1), dimensions={0}, to_apply=%region_0.1 | reduce | flops 6422528 | bytes 33030148 | tf_op jit(solution)/shard_map/reduce_sum | solution.py:55
  366.3 5.2 copy.7
  371.5 3.7 fusion.163
  375.4 1.7 copy-done
  378.0 2.1 fusion.39
  380.1 1.9 fusion.63
  382.1 2.1 fusion.87
  384.2 1.9 fusion.111
  386.1 2.0 fusion.45
  393.1 25.3 %all_to_all.10 = f32[16,64,256]{2,1,0:T(8,128)S(1)} all-to-all(f32[16,64,256]{2,1,0:T(8,128)S(1)} %bitcast.113), channel_id=1, replica_groups=mesh['tok'=8,'row'=4,'col'=4] {'row','col'}, dimensions={0} | all-to-all | bytes 2097152 | tf_op jit(solution)/shard_map/all_to_all | solution.py:21
  419.2 4.2 all-to-all-start.1
  423.4 6.8 %all-to-all-done.1 = f32[4,64,256]{2,1,0:T(8,128)S(1)} async-done(((f32[4,64,256]{2,1,0:T(8,128)}), f32[4,64,256]{2,1,0:T(8,128)S(1)}, u32[]{:S(2)}, u32[]{:S(2)}) %all-to-all-start.1) | async-done | bytes 262176 | tf_op jit(solution)/shard_map/all_to_all | solution.py:33
  430.2 8.2 %all-gather.7.cloned.1.call-done = f32[16,256,256]{2,1,0:T(8,128)} async-done(((f32[1,256,256]{2,1,0:T(8,128)}), f32[16,256,256]{2,1,0:T(8,128)}) %all-gather.7.cloned.1.call-update) | async-done | bytes 4194320 | tf_op jit(solution)/shard_map/all_gather | solution.py:10
  438.4 1.0 dynamic_slice.70
  439.5 1.0 fusion.150
  440.5 11.7 %cholesky.50 = f32[128,128]{1,0:T(8,128)S(1)} custom-call(f32[128,128]{1,0:T(8,128)S(1)} %cholesky.118), custom_call_target="Cholesky" | custom-call | tf_op jit(solution)/shard_map/jit(cholesky)/cholesky | solution.py:75
  452.3 9.8 %custom-call.16 = f32[1,128,128]{1,2,0:T(8,128)S(1)} custom-call(f32[1,128,128]{2,1,0:T(8,128)S(1)} %get-tuple-element.27), custom_call_target="InvertDiagBlocksLowerTriangular" | custom-call | tf_op jit(solution)/shard_map/jit(cholesky)/cholesky | solution.py:75
  462.6 11.7 %cholesky.105 = f32[128,128]{1,0:T(8,128)S(1)} custom-call(f32[128,128]{1,0:T(8,128)S(1)} %convolution_subtract_fusion.2), custom_call_target="Cholesky" | custom-call | tf_op jit(solution)/shard_map/jit(cholesky)/cholesky | solution.py:75
  476.4 4.2 while.1
  477.3 1.3 bitcast_dynamic-update-slice_fusion.2
  479.3 1.3 bitcast_dynamic-update-slice_fusion.2
  480.7 19.7 %custom-call.17 = f32[2,128,128]{1,2,0:T(8,128)S(1)} custom-call(f32[2,128,128]{2,1,0:T(8,128)S(1)} %get-tuple-element.9), custom_call_target="InvertDiagBlocksLowerTriangular" | custom-call | tf_op jit(solution)/shard_map/triangular_solve | solution.py:81
  501.3 10.1 %all_gather.27 = f32[64,1024]{1,0:T(8,128)} all-gather(f32[64,256]{1,0:T(8,128)S(1)} %fusion.153), channel_id=1, replica_groups=mesh['tok'=8,'row'=4,'col'=4] {'col'}, dimensions={1}, use_global_device_ids=true | all-gather | bytes 327680 | tf_op jit(solution)/shard_map/all_gather | solution.py:83
  511.4 2.2 fusion.175
  513.7 1.0 fusion.132
  514.7 1.0 convolution_subtract_fusion
  516.6 17.3 %all-gather.9.cloned.1.call-done = f32[256,1024]{1,0:T(8,128)} async-done(((f32[64,1024]{1,0:T(8,128)}), f32[256,1024]{1,0:T(8,128)}) %all-gather.9.cloned.1.call-update) | async-done | bytes 1048592 | tf_op jit(solution)/shard_map/all_gather | solution.py:86
  533.9 8.7 %convolution_convert_fusion = bf16[1792,1024]{1,0:T(8,128)(2,1)} fusion(f32[256,1024]{1,0:T(8,128)} %all-gather.9.cloned.1.call-done, f32[1792,128]{0,1:T(8,128)S(1)} %fusion.158, f32[1792,128]{0,1:T(8,128)S(1)} %fusion.132), kind=kOutput, calls=%fused_computation.2 | convolution fusion | flops 5639438336 | bytes 6553600 | tf_op jit(solution)/shard_map/dot_general | solution.py:84
  (58 shorter events, 11.9 us)
Async XLA Ops:
  7.2 55.7 %all-gather.11.cloned.1.call-start = ((), (), s32[]{:S(2)}) async-start(), calls=%async_computation.4 | async-start | bytes 2228224 | tf_op jit(solution)/shard_map/all_gather | solution.py:10
  8.8 344.7 %all-gather.13.cloned.1.call-start = ((), (), s32[]{:S(2)}) async-start(), calls=%async_computation.5 | async-start | bytes 33030144 | tf_op jit(solution)/shard_map/all_gather | solution.py:55
  66.6 371.8 %all-gather.7.cloned.1.call-start = ((), (), s32[]{:S(2)}) async-start(), calls=%async_computation.2 | async-start | bytes 4456448 | tf_op jit(solution)/shard_map/all_gather | solution.py:10
  375.2 1.9 copy-start
  375.2 2.8 copy-start.1
  378.0 10.1 %slice-start = ((s8[7340032]{0:T(1024)(128)(4,1)}), s8[4194304]{0:T(1024)(128)(4,1)S(1)}, s32[]{:S(2)}) async-start(s8[7340032]{0:T(1024)(128)(4,1)} %bitcast.116), calls=%async_computation.6 | async-start | bytes 8388608
  382.1 6.1 %slice-start.1 = ((s8[7340032]{0:T(1024)(128)(4,1)}), s8[3145728]{0:T(1024)(128)(4,1)S(1)}, s32[]{:S(2)}) async-start(s8[7340032]{0:T(1024)(128)(4,1)} %bitcast.116), calls=%async_computation.7 | async-start | bytes 6291456
  419.2 11.0 %all-to-all-start.1 = ((f32[4,64,256]{2,1,0:T(8,128)}), f32[4,64,256]{2,1,0:T(8,128)S(1)}, u32[]{:S(2)}, u32[]{:S(2)}) async-start(f32[4,64,256]{2,1,0:T(8,128)} %broadcast_in_dim.21), calls=%async_computation.1 | async-start | bytes 524288 | tf_op jit(solution)/shard_map/all_to_all | solution.py:33
  423.4 110.5 %all-gather.9.cloned.1.call-start = ((), (), s32[]{:S(2)}) async-start(), calls=%async_computation.3 | async-start | bytes 1310720 | tf_op jit(solution)/shard_map/all_gather | solution.py:86
  501.3 12.4 %copy-start.2 = (f32[64,256]{1,0:T(8,128)}, f32[64,256]{1,0:T(8,128)S(1)}, u32[]{:S(2)}) copy-start(f32[64,256]{1,0:T(8,128)S(1)} %fusion.153) | copy-start | bytes 196612
Sparse Core Ops, SparseCore 0:
  11.0 51.8 all-gather.10
  66.8 286.6 all-gather.12
  378.1 60.3 all-gather.6
  511.6 22.2 all-gather.8
